TPU v7x, 32 devices: a 4x4x1 block of a 4x4x8 slice. The times are simulated.
32 devices in a mesh: dp: 1 (over z), row: 4 (over y), col: 8 (over x, core).
Axes of the slice: x: 4, y: 4, z: 1, core: 2. Of those that a mesh axis runs over, the one named last changes fastest.
The devices are a block of a 4x4x8 slice.
Arguments:
- x_in: bfloat16 [16, 512, 2560], P('dp', None, ('row', 'col'))
- ln_gain: bfloat16 [2, 2560], P(None, ('row', 'col'))
- w_in: bfloat16 [2, 2560, 23040], P(None, 'row', 'col')
- w_kv: bfloat16 [2, 2560, 160], P(None, 'row', 'col')
- w_out: bfloat16 [2, 12800, 2560], P(None, 'col', 'row')
Outputs:
- output 1: bfloat16 [16, 512, 2560], P('dp', None, ('row', 'col'))
- output 2: bfloat16 [2, 2, 16, 512, 80], P(None, None, 'dp', ('row', 'col'))
All inputs are finite; a program needn't handle non-finite values.
Results may differ from a plain program's by a relative error of at most 0.0163933.
Values are sent between devices in bfloat16 or wider.
A program may use at most 768 MiB of HBM per device.

v0:
```python
import functools

import numpy as np

import jax
import jax.numpy as jnp
from jax import lax
from jax.experimental import pallas as pl
from jax.experimental.pallas import tpu as pltpu
from jax.sharding import PartitionSpec as P

LN_EPS = 1e-6
MESH = pl.DeviceIdType.MESH
ANY = pl.BlockSpec(memory_space=pl.ANY)
VMEM = pl.BlockSpec(memory_space=pltpu.VMEM)
F32, BF16 = jnp.float32, jnp.bfloat16


def dot(a, b):
    return jnp.dot(a, b, preferred_element_type=F32)


class Dims:
    pass


def rows_at(start, count, by=16):
    return pl.ds(start if isinstance(start, int) else pl.multiple_of(start, by), count)


def kernel(
    D,
    x_t, gains, w_t, wkv_t, w_o, cos_ref, sin_ref, perm_ref,
    y_out, kv_out, g_w, g_kv, g_wo, g_h,
    xland, gland, gcol, hid, ht, wbuf, wonat, wobuf, qt, kvland, kn, vt, kvbuf, jt, ot, twin_in, far_in, near_in, psum, pair_in,
    xs, xr, gs, gr, ys, yr, ags, agr, ps, pr_, kvs, kvr, rss, rsr, es, er, lw, lo, lh, fs, fr, fl,
):
    sc = jax.named_scope
    row, col = lax.axis_index("row"), lax.axis_index("col")
    n_row, n_col, n = D.n_row, D.n_col, D.n_row * D.n_col
    n_x = n_col // 2
    me = row * n_col + col
    x, k = col // 2, lax.rem(col, 2)
    xr_, xl_, xf_ = lax.rem(x + 1, n_x), lax.rem(x + n_x - 1, n_x), lax.rem(x + 2, n_x)
    right, left, twin = xr_ * 2 + k, xl_ * 2 + k, x * 2 + 1 - k
    up, down, across = lax.rem(row + 1, n_row), lax.rem(row + n_row - 1, n_row), lax.rem(row + 2, n_row)
    half, mate = row // 2, n_row - 1 - row
    peer = row + 1 - 2 * lax.rem(row, 2)
    tok, dl, dr = D.tok, D.dl, D.dr
    och, fch = D.och, D.fch
    my_lanes = pl.ds(pl.multiple_of(k * tok, 128), tok)
    twin_lanes = pl.ds(pl.multiple_of((1 - k) * tok, 128), tok)

    def remote(src, dst, ssem, rsem, r, c):
        return pltpu.make_async_remote_copy(src_ref=src, dst_ref=dst, send_sem=ssem, recv_sem=rsem, device_id={"row": r, "col": c}, device_id_type=MESH)

    def loop(lo_, hi_, f):
        def body(i, carry):
            f(i)
            return carry

        lax.fori_loop(lo_, hi_, body, 0)

    barrier = pltpu.get_barrier_semaphore()

    def greet(i):
        d = lax.rem(me + i, n)
        pl.semaphore_signal(barrier, inc=1, device_id={"row": d // n_col, "col": lax.rem(d, n_col)}, device_id_type=MESH)

    with sc("barrier"):
        loop(1, n, greet)
        pl.semaphore_wait(barrier, n - 1)

    def piece_of(ref, d):
        return ref.at[d // 2, :, pl.ds(pl.multiple_of(lax.rem(d, 2) * tok, 128), tok)]

    def x_copy(i):
        d = lax.rem(me + i, n)
        return remote(piece_of(x_t, d), xland.at[me], xs.at[i], xr.at[i], d // n_col, lax.rem(d, n_col))

    def g_copy(i):
        d = lax.rem(me + i, n)
        return remote(gains, gland.at[me], gs.at[i], gr.at[i], d // n_col, lax.rem(d, n_col))

    own_x = pltpu.make_async_copy(piece_of(x_t, me), xland.at[me], xr.at[0])
    own_g = pltpu.make_async_copy(gains, gland.at[me], gr.at[0])
    own_x.start()
    own_g.start()
    def x_first(i):
        x_copy(i).start()
        g_copy(i).start()

    loop(1, n, x_first)

    def own_lanes(r):
        return pl.ds(pl.multiple_of(r * dr, 128), dr)

    def o_lanes(j, r):
        return pl.ds(pl.multiple_of(lax.rem(r + j, D.n_o) * och, 128), och)

    steps = []
    for l, C in enumerate(D.cfg):
        steps += [(l, "q", 0)] + [(l, "f", j) for j in range(C.n_f)] + [(l, "o", j) for j in range(D.n_o)]
    n_steps = len(steps)
    step_of = {s: t for t, s in enumerate(steps)}

    def blocks(t, i):
        l, kind, j = steps[t]
        C = D.cfg[l]
        out = []

        def w_rows(a, m):
            at = rows_at(a, m)
            out.append((w_t.at[l, at, :], lambda r: g_w.at[l, at, own_lanes(r)]))

        def o_rows(a, m):
            at = rows_at(a, m)
            out.append((w_o.at[l, at, o_lanes(j, row)], lambda r: g_wo.at[l, r, at, o_lanes(j, r)]))

        def kv_rows(a, m):
            at = pl.ds(a, m)
            out.append((wkv_t.at[l, at, :], lambda r: g_kv.at[l, at, own_lanes(r)]))

        if kind == "q":
            for a in (0, C.q // 2):
                w_rows(i * C.q + a, C.q // 2)
            for a in (0, D.kvp // 2):
                kv_rows(a, D.kvp // 2)
        elif kind == "f":
            w_rows(D.q + i * C.f + j * fch, fch)
            w_rows(D.q + D.f + i * C.f + j * fch, fch)
        elif C.split:
            o_rows(i * C.q, C.q)
            o_rows(D.q + i * C.f, C.f)
        else:
            for a in (0, (D.q + D.f) // 2):
                o_rows(a, (D.q + D.f) // 2)
        return out

    base, n_sems = [], 0
    for l, kind, j in steps:
        base.append(n_sems)
        n_sems += 12 if kind == "q" else 6
    assert n_sems == ys.shape[0]
    y_sent = []

    def y_copy(t, i, kind, src, dst, r):
        at = base[t] + 3 * i + kind
        return remote(src, dst, ys.at[at], yr.at[at], r, col)

    def y_send(*args):
        c = y_copy(*args)
        c.start()
        y_sent.append(c)

    def issue_peer(t):
        for i, (src, place) in enumerate(blocks(t, half if D.cfg[steps[t][0]].split else 0)):
            y_send(t, i, 0, src, place(row), peer)

    def issue_mate(t):
        for i, (src, place) in enumerate(blocks(t, 1 - half if D.cfg[steps[t][0]].split else 0)):
            y_send(t, i, 1, src, place(row), mate)

    def relay(t):
        split = D.cfg[steps[t][0]].split
        with sc(f"relay{t}"):
            for i, (src, place) in enumerate(blocks(t, half if split else 0)):
                y_copy(t, i, 1, src, place(mate), mate).wait_recv()
                if split or i % 2 == 0:
                    y_send(t, i, 2, place(mate), place(mate), peer)
                if not split:
                    y_copy(t, i, 0, src, place(peer), peer).wait_recv()
                    if i % 2 == 1:
                        y_send(t, i, 2, place(peer), place(peer), mate)

    at = {"next": 0, "peer": 0, "mate": 0, "relay": 0}
    first_of = {l: min(t for t, st in enumerate(steps) if st[0] == l) for l in range(D.layers)}

    def step(l, j):
        return min(first_of[l] + j, first_of.get(l + 1, n_steps) - 1)

    def peer_to(t):
        while at["peer"] <= t:
            issue_peer(at["peer"])
            at["peer"] += 1

    def mate_to(t):
        while at["mate"] <= t:
            issue_mate(at["mate"])
            at["mate"] += 1

    def relay_to(t):
        assert t < at["peer"] and t < at["mate"]
        while at["relay"] <= t:
            relay(at["relay"])
            at["relay"] += 1

    def advance():
        t = at["next"]
        assert t < at["relay"], t
        rest = n_row - 1 - peer
        with sc(f"adv{t}"):
            split = D.cfg[steps[t][0]].split
            for i, (src, place) in enumerate(blocks(t, half if split else 0)):
                if split:
                    y_copy(t, i, 0, src, place(peer), peer).wait_recv()
                y_copy(t, i, 2, src, place(rest), rest).wait_recv()
            at["next"] = t + 1

    def have(*which):
        while at["next"] <= step_of[which]:
            advance()

    mate_to(1)
    peer_to(step(0, 3))

    def w_fetch(l, kind, j, slot):
        C = D.cfg[l]
        i = half if C.split else 0
        copies = []

        def fetch(src, dst):
            copies.append(pltpu.make_async_copy(src, dst, lw.at[slot, len(copies)]))

        def w_rows(a, m, at):
            a, at = rows_at(a, m), pl.ds(at, m)
            fetch(w_t.at[l, a, :], wbuf.at[slot, at, own_lanes(row)])
            for r in (up, down, across):
                fetch(g_w.at[l, a, own_lanes(r)], wbuf.at[slot, at, own_lanes(r)])

        if kind == "q":
            w_rows(i * C.q, C.q, 0)
            at = pl.ds(C.q, D.kvp)
            fetch(wkv_t.at[l], wbuf.at[slot, at, own_lanes(row)])
            for r in (up, down, across):
                fetch(g_kv.at[l, :, own_lanes(r)], wbuf.at[slot, at, own_lanes(r)])
        else:
            w_rows(D.q + i * C.f + j * C.cw, C.cw, 0)
            w_rows(D.q + D.f + i * C.f + j * C.cw, C.cw, C.cw)
        return copies

    def o_fetch(l, j, slot):
        C = D.cfg[l]
        copies = []

        def fetch(src, dst):
            copies.append(pltpu.make_async_copy(src, dst, lo.at[slot, len(copies)]))

        spans = ((half * C.q, 0, C.q), (D.q + half * C.f, C.q, C.f)) if C.split else ((0, 0, C.q + C.f),)
        for a, at, m in spans:
            a, at = rows_at(a, m), pl.ds(at, m)
            to = lambda r: pl.ds(pl.multiple_of(r * och, 128), och)
            fetch(w_o.at[l, a, o_lanes(j, row)], wonat.at[slot, at, to(row)])
            for r in (up, down, across):
                fetch(g_wo.at[l, r, a, o_lanes(j, r)], wonat.at[slot, at, to(r)])
        return copies

    def start(copies):
        for c in copies:
            c.start()

    def wait(copies):
        for c in copies:
            c.wait()

    own_x.wait()
    own_g.wait()

    def x_finish(i):
        s = lax.rem(me + n - i, n)
        remote(xland.at[s], xland.at[s], xs.at[i], xr.at[i], row, col).wait_recv()
        remote(gland.at[s], gland.at[s], gs.at[i], gr.at[i], row, col).wait_recv()
        x_copy(i).wait_send()
        g_copy(i).wait_send()

    with sc("xwait"):
        loop(1, n, x_finish)

    def keep(d):
        hid[rows_at(d * dl, dl), :] = xland[d]

    with sc("gains"):
        loop(0, n, keep)
        g_all = gland[...].astype(F32)
        for l in range(D.layers):
            g_rows = g_all[:, l, :]
            g_rows = jnp.concatenate([g_rows, jnp.zeros((128 - n, 128), F32)], axis=0) if n < 128 else g_rows
            g_cols = g_rows.T
            for d in range(n):
                gcol[l, d * dl : (d + 1) * dl, :] = jnp.broadcast_to(g_cols[:dl, d : d + 1], (dl, 128))

    blk = 64
    n_blk = D.d // blk

    def layer_norm(l):
        def add_up(i, acc):
            v = hid[rows_at(i * blk, blk), :].astype(F32)
            return acc + v.reshape(blk // 8, 8, tok).sum(axis=0)

        mean = lax.fori_loop(0, n_blk, add_up, jnp.zeros((8, tok), F32)).sum(axis=0, keepdims=True) / D.d

        def add_sq(i, acc):
            v = hid[rows_at(i * blk, blk), :].astype(F32) - mean
            return acc + (v * v).reshape(blk // 8, 8, tok).sum(axis=0)

        var = lax.fori_loop(0, n_blk, add_sq, jnp.zeros((8, tok), F32)).sum(axis=0, keepdims=True) / D.d
        scale = lax.rsqrt(var + LN_EPS)

        def write(i):
            rows = rows_at(i * blk, blk)
            g = gcol[l, rows, :]
            g = jnp.concatenate([g] * (tok // 128), axis=1)
            v = (hid[rows, :].astype(F32) - mean) * scale * g
            ht[x, rows, my_lanes] = v.astype(BF16)

        with sc(f"norm{l}"):
            loop(0, n_blk, write)

    d_low, d_high = pl.ds(0, D.d // 2), pl.ds(D.d // 2, D.d // 2)

    class Gather:
        def __init__(self, ref, tag):
            self.ref, self.tag, self.sends = ref, tag, []
            for i, part, c in ((0, 0, right), (1, 0, left), (2, None, twin), (9, 1, right), (10, 1, left)):
                self.send(i, ref(x, False, part), c)

        def send(self, i, ref, c):
            copy = remote(ref, ref, ags.at[self.tag, i], agr.at[self.tag, i], row, c)
            copy.start()
            self.sends.append(copy)

        def arrived(self, i, ref):
            remote(ref, ref, ags.at[self.tag, i], agr.at[self.tag, i], row, col).wait_recv()

        def pass_low(self):
            with sc(f"pass_low{self.tag}"):
                self.arrived(0, self.ref(xl_, False, 0))
                self.send(3, self.ref(xl_, False, 0), right)
                self.send(4, self.ref(xl_, False, 0), twin)
                self.arrived(1, self.ref(xr_, False, 0))
                self.send(6, self.ref(xr_, False, 0), twin)

        def pass_on(self):
            with sc(f"pass_on{self.tag}"):
                self.arrived(10, self.ref(xr_, False, 1))
                self.send(5, self.ref(xr_, False, 1), left)
                self.send(12, self.ref(xr_, False, 1), twin)
                self.arrived(9, self.ref(xl_, False, 1))
                self.send(11, self.ref(xl_, False, 1), twin)

        def own(self):
            with sc(f"own{self.tag}"):
                self.arrived(2, self.ref(x, True, None))

        def near(self):
            with sc(f"near{self.tag}"):
                self.arrived(4, self.ref(xl_, True, 0))
                self.arrived(6, self.ref(xr_, True, 0))
                self.arrived(12, self.ref(xr_, True, 1))
                self.arrived(11, self.ref(xl_, True, 1))

        def pass_far(self):
            with sc(f"pass_far{self.tag}"):
                for part, i, j in ((0, 3, 7), (1, 5, 8)):
                    self.arrived(i, self.ref(xf_, False, part))
                    self.send(j, self.ref(xf_, False, part), twin)

        def far(self):
            with sc(f"far{self.tag}"):
                self.arrived(7, self.ref(xf_, True, 0))
                self.arrived(8, self.ref(xf_, True, 1))

        def finish(self):
            for c in self.sends:
                c.wait_send()

    def normed_of(buf):
        def ref(chip, other, part):
            rows = slice(None) if part is None else (d_low, d_high)[part]
            return buf.at[chip, rows, twin_lanes if other else my_lanes]

        return ref

    def kv_of(a):
        def ref(chip, other, part):
            h = D.seqs // 2
            span = pl.ds(a * D.seqs, D.seqs) if part is None else pl.ds(a * D.seqs + part * h, h)
            return kvland.at[chip * 2 + (1 - k if other else k), span]

        return ref

    half_dim = D.hd // 2

    def near3(i):
        return lax.rem(x + i + i // 2, n_x)

    def all4(i):
        return i

    def far1(i):
        return xf_

    def rope(p):
        lo_, hi_ = p[:half_dim], p[half_dim:]
        return jnp.concatenate([lo_ * cos_ref[...] - hi_ * sin_ref[...], hi_ * cos_ref[...] + lo_ * sin_ref[...]], axis=0)

    def project_q(l, a, seq_of, count):
        C = D.cfg[l]

        def body(i):
            s = seq_of(i)
            p = dot(wbuf[1, : C.q + D.kvp, :], ht[s]).astype(BF16).astype(F32)
            for h in range(C.heads):
                at = rows_at((a * D.seqs + s) * C.q + h * D.hd, D.hd)
                qt[at, :] = (rope(p[h * D.hd : (h + 1) * D.hd]) * D.hd**-0.5).astype(BF16)
            kvland[col, a * D.seqs + s] = p[C.q :].astype(BF16)

        with sc(f"q{l}{a}"):
            loop(0, count, body)

    def kv_copy(s, j, source):
        ref = kvland.at[source, s]
        return remote(ref, ref, kvs.at[s, j], kvr.at[s, j], row, lax.rem(col + j, n_col))

    def kv_send(seq_of, count):
        def body(i):
            s = seq_of(i)
            loop(1, n_col, lambda j: kv_copy(s, j, col).start())

        loop(0, count, body)

    def kv_arrive():
        def body(i):
            j = i // D.seqs + 1
            s = lax.rem(i, D.seqs)
            kv_copy(s, j, lax.rem(col + n_col - j, n_col)).wait_recv()
            kv_copy(s, j, col).wait_send()

        with sc("kvwait"):
            loop(0, D.seqs * (n_col - 1), body)

    def key_value(l, a):
        def body(i):
            s = a * D.seqs + i
            raw = kvland[:, s].reshape(n_col * D.kvp, D.seq)
            both = dot(perm_ref[...], raw)
            zeros = jnp.zeros((128 - D.hd, D.seq), F32)
            k_nat = jnp.concatenate([rope(both[: D.hd]), zeros], axis=0).T.astype(BF16)
            kn[s] = k_nat
            vt[s] = both[D.hd :].astype(BF16)
            if a == 0:
                kvbuf[l, 0, i] = k_nat
                kvbuf[l, 1, i] = jnp.concatenate([both[D.hd :], zeros], axis=0).T.astype(BF16)

        with sc(f"kv{l}{a}"):
            loop(0, D.seqs, body)

    qb = D.seq // 2

    def attention(l, a):
        C = D.cfg[l]

        pair = 2
        per = C.heads // pair

        def body(i):
            s, h0 = a * D.seqs + i // per, lax.rem(i, per) * pair
            q_rows = [rows_at(s * C.q + (h0 + e) * D.hd, D.hd) for e in range(pair)]
            o_rows = [rows_at(s * (C.q + C.f) + (h0 + e) * D.hd, D.hd) for e in range(pair)]
            for b in range(2):
                ext = (b + 1) * qb
                lanes = slice(b * qb, (b + 1) * qb)
                keys = lax.broadcasted_iota(jnp.int32, (ext, qb), 0)
                queries = lax.broadcasted_iota(jnp.int32, (ext, qb), 1) + b * qb
                scores = [dot(kn[s, :ext, : D.hd], qt[q_rows[e], lanes]) for e in range(pair)]
                for e in range(pair):
                    score = jnp.where(keys <= queries, scores[e], -1e30)
                    p = jnp.exp(score - jnp.max(score, axis=0, keepdims=True))
                    p = (p * (1.0 / jnp.sum(p, axis=0, keepdims=True))).astype(BF16)
                    jt[o_rows[e], lanes] = dot(vt[s, :, :ext], p).astype(BF16)

        with sc(f"attn{l}{a}"):
            loop(0, D.seqs * per, body)

    def gate_up(l, a, slot, j, seq_of, count):
        C = D.cfg[l]

        def body(i):
            s = seq_of(i)
            p = dot(wbuf[slot, : 2 * C.cw, :], ht[s])
            g = p[: C.cw].astype(BF16).astype(F32)
            u = p[C.cw :].astype(BF16).astype(F32)
            jt[rows_at((a * D.seqs + s) * (C.q + C.f) + C.q + j * C.cw, C.cw), :] = (g * jax.nn.sigmoid(g) * u).astype(BF16)

        loop(0, count, body)

    def gate_up_loop(l, a, seq_of, count, first, last, stop=None):
        C = D.cfg[l]
        stop = C.n_c if stop is None else stop
        have_chunk(l, min(last, stop - 1))

        def body(j):
            slot = lax.rem(j, 2)
            wait(w_fetch(l, "f", j, slot))

            @pl.when(j + 1 < stop)
            def _():
                start(w_fetch(l, "f", j + 1, 1 - slot))

            gate_up(l, a, slot, j, seq_of, count)

        with sc(f"gu{l}{a}"):
            loop(first, last, body)

    def have_chunk(l, j):
        C = D.cfg[l]
        have(l, "f", (j + 1) * C.cw // fch - 1)

    def load_q(l):
        have(l, "q", 0)
        copies = w_fetch(l, "q", 0, 1)
        start(copies)
        wait(copies)

    m = och * n_row
    m_low, m_high = pl.ds(0, m // 2), pl.ds(m // 2, m // 2)
    r_slots = twin_in.shape[0]
    r_step = 64

    def order(i):
        return lax.rem(x + lax.rem(2 + 3 * i, 4), n_x)

    class Reduce:
        def __init__(self, l):
            self.l, self.C, self.sends = l, D.cfg[l], {}

        def send(self, u, i, src, dst, c):
            copy = remote(src, dst, rss.at[u % r_slots, i], rsr.at[u % r_slots, i], row, c)
            copy.start()
            self.sends[u].append(copy)

        def arrived(self, u, i, ref):
            remote(ref, ref, rss.at[u % r_slots, i], rsr.at[u % r_slots, i], row, col).wait_recv()

        def twin_copy(self, u, i):
            us = u % r_slots
            return remote(ot.at[u % 2, order(i), :, twin_lanes], twin_in.at[us, i], rss.at[us, i], rsr.at[us, i], row, twin)

        def twin_done(self, u):
            loop(0, 4, lambda i: self.twin_copy(u, i).wait_send())

        def stage_a(self, u, a):
            C = self.C
            if u >= 2:
                self.twin_done(u - 2)
            if u >= r_slots - 1:
                for c in self.sends.pop(u - r_slots + 1):
                    c.wait_send()
            self.sends[u] = []
            R = C.q + C.f

            def body(i):
                s = order(i)
                ot[u % 2, s] = dot(wobuf[:, :R], jt[rows_at((a * D.seqs + s) * R, R), :]).astype(BF16)
                self.twin_copy(u, i).start()

            with sc(f"sa{self.l}_{u}"):
                loop(0, 4, body)

        def stage_b(self, u):
            us = u % r_slots

            def body(i):
                self.arrived(u, i, twin_in.at[us, i])
                s = order(i)

                def add(b):
                    at = rows_at(b * r_step, r_step)
                    twin_in[us, i, at, :] = (ot[u % 2, s, at, my_lanes].astype(F32) + twin_in[us, i, at, :].astype(F32)).astype(BF16)

                loop(0, m // r_step, add)

            far = [
                remote(twin_in.at[us, 0, m_low], far_in.at[us, m_low], rss.at[us, 4], rsr.at[us, 4], row, right),
                remote(twin_in.at[us, 0, m_high], far_in.at[us, m_high], rss.at[us, 5], rsr.at[us, 5], row, left),
            ]
            self.sends[u] += far

            def each(i):
                body(i)

                @pl.when(i == 0)
                def _():
                    start(far)

            with sc(f"sb{self.l}_{u}"):
                loop(0, 4, each)

        def stage_c(self, u):
            us = u % r_slots

            def add_far(i, base):
                def add(b):
                    at = rows_at(base + b * r_step, r_step)
                    twin_in[us, i, at, :] = (twin_in[us, i, at, :].astype(F32) + far_in[us, at, :].astype(F32)).astype(BF16)

                loop(0, m // 2 // r_step, add)

            with sc(f"sc{self.l}_{u}"):
                self.arrived(u, 4, far_in.at[us, m_low])
                add_far(1, 0)
                self.send(u, 6, twin_in.at[us, 1], near_in.at[us, 0], right)
                self.arrived(u, 5, far_in.at[us, m_high])
                add_far(3, m // 2)
                self.send(u, 7, twin_in.at[us, 3], near_in.at[us, 1], left)

        def add_update(self, j, total):
            step = min(r_step, och)
            for r in range(n_row):

                def add(b, r=r):
                    dst = rows_at(r * dr + (r + j) % D.n_o * och + b * step, step)
                    u = total(rows_at(r * och + b * step, step)).astype(BF16).astype(F32)
                    hid[dst, :] = (hid[dst, :].astype(F32) + u).astype(BF16)

                loop(0, och // step, add)

        def stage_d(self, u, j, a):
            us = u % r_slots

            def total(at):
                return twin_in[us, 2, at, :].astype(F32) + near_in[us, 0, at, :].astype(F32) + near_in[us, 1, at, :].astype(F32)

            with sc(f"sd{self.l}_{u}"):
                self.arrived(u, 6, near_in.at[us, 0])
                self.arrived(u, 7, near_in.at[us, 1])
                if self.C.split:

                    def save(b):
                        at = rows_at(b * r_step, r_step)
                        psum[a, j, at, :] = total(at).astype(BF16)

                    loop(0, m // r_step, save)
                    if a == 1:
                        remote(psum.at[1, j], pair_in.at[j], es.at[j], er.at[j], mate, col).start()
                else:
                    self.add_update(j, total)

        def stage_e(self, j):
            with sc(f"se{self.l}_{j}"):
                c = remote(psum.at[1, j], pair_in.at[j], es.at[j], er.at[j], mate, col)
                c.wait_recv()
                self.add_update(j, lambda at: psum[0, j, at, :].astype(F32) + pair_in[j, at, :].astype(F32))
                c.wait_send()

        def finish(self, units):
            with sc(f"rfin{self.l}"):
                for u in range(max(0, units - 2), units):
                    self.twin_done(u)
                for u in self.sends:
                    for c in self.sends[u]:
                        c.wait_send()

    o_started = set()

    def o_load(l, j, a):
        if (l, j, a) not in o_started:
            have(l, "o", j)
            start(o_fetch(l, j, j % 2))
            o_started.add((l, j, a))

    def o_use(l, j, a):
        C = D.cfg[l]
        with sc(f"ouse{l}_{j}"):
            o_load(l, j, a)
            wait(o_fetch(l, j, j % 2))
            R = C.q + C.f
            for r in range(n_row):
                wobuf[r * och : (r + 1) * och, :R] = wonat[j % 2, :R, r * och : (r + 1) * och].T

    layer_norm(0)
    g0 = Gather(normed_of(ht), 0)
    mine = ht.at[x, :, my_lanes]
    shared = g_h.at[x, :, my_lanes]
    to_mate = remote(mine, shared, ps, pr_, mate, col)
    to_mate.start()
    relay_to(1)
    mate_to(step(0, 5))
    peer_to(step(0, 5))
    g0.pass_low()
    g0.pass_on()
    with sc("mate"):
        to_mate.wait_recv()
    g1 = Gather(normed_of(g_h), 1)
    load_q(0)
    g0.own()
    g0.near()
    project_q(0, 0, near3, 3)
    relay_to(2)
    mate_to(step(0, 10))
    g0.pass_far()
    g0.far()
    project_q(0, 0, far1, 1)
    kv0 = Gather(kv_of(0), 2)
    relay_to(3)
    n_f = D.cfg[0].n_f
    f_started = set()

    def f_load(j):
        if j not in f_started:
            f_started.add(j)
            start(w_fetch(0, "f", j, j % 2))

    def h_copy(i):
        return pltpu.make_async_copy(g_h.at[i], ht.at[i], lh.at[i])

    have(0, "f", 0)
    f_load(0)
    gate_up_loop(0, 0, all4, 4, 0, 2, 2)
    relay_to(step(0, 4))
    for j in range(2, n_f):
        have(0, "f", j)
        f_load(j)
        with sc(f"gu0_{j}"):
            wait(w_fetch(0, "f", j, j % 2))
            gate_up(0, 0, j % 2, j, all4, 4)
        if j == max(2, n_f - 3):
            relay_to(step(0, 5))
            peer_to(step(0, 6))
            relay_to(step(0, 6))
            peer_to(step(0, 7))
    kv0.pass_low()
    kv0.pass_on()
    g1.pass_low()
    g1.pass_on()
    for t in (7, 8):
        relay_to(step(0, t))
        peer_to(step(0, t + 1))
    relay_to(step(0, 9))
    peer_to(step(0, 10))
    relay_to(step(0, 10))
    peer_to(step(1, 5))
    mate_to(step(1, D.cfg[1].n_f - 2))
    g0.finish()
    to_mate.wait_send()
    g1.own()
    g1.near()
    loop(0, 3, lambda i: h_copy(near3(i)).start())
    kv0.pass_far()
    with sc("kv0wait"):
        kv0.own()
        kv0.near()
        kv0.far()
        kv0.finish()
    key_value(0, 0)
    attention(0, 0)

    red = Reduce(0)
    units = [(j, 0) for j in range(D.n_o - 1)] + [(j, 1) for j in range(D.n_o)] + [(D.n_o - 1, 0)]
    n_u = len(units)
    first = D.n_o - 1
    state = {"e": 0}

    def settle(count):
        while state["e"] < count:
            red.stage_e(state["e"])
            state["e"] += 1

    def unit(u):
        j, a = units[u]
        if u == 0 or units[u - 1][0] != j:
            o_use(0, j, a)
        red.stage_a(u, a)
        if u + 1 < n_u and units[u + 1][0] != j:
            o_load(0, *units[u + 1])
        if u >= 2:
            red.stage_c(u - 2)
        if u >= 3:
            red.stage_d(u - 3, *units[u - 3])
        red.stage_b(u)

    unit(0)
    g1.pass_far()
    unit(1)
    g1.far()
    h_copy(xf_).start()
    load_q(0)
    start(w_fetch(0, "f", 0, 0))
    loop(0, 3, lambda i: h_copy(near3(i)).wait())
    h_copy(xf_).wait()
    project_q(0, 1, all4, 4)
    kv1 = Gather(kv_of(1), 3)
    parts = first - 2
    cuts = [n_f * i // parts for i in range(parts + 1)]
    for u in range(2, first):
        unit(u)
        if u == 2:
            kv1.pass_low()
            kv1.pass_on()
        gate_up_loop(0, 1, all4, 4, cuts[u - 2], cuts[u - 1])
    kv1.pass_far()
    relay_to(step(1, 1))
    with sc("kv1wait"):
        kv1.own()
        kv1.near()
        kv1.far()
        kv1.finish()
    key_value(0, 1)
    attention(0, 1)
    g1.finish()
    relay_to(step(1, 2))
    peer_to(step(1, 7))
    n_f1 = D.cfg[1].n_f
    for u in range(first, n_u):
        unit(u)
        v = u - first
        if v in (0, 1, 2):
            relay_to(step(1, min(v + 3, n_f1 - 2)))
        if v == 1:
            peer_to(step(1, min(8, n_f1)))
        elif v == 4:
            peer_to(step(1, min(9, n_f1)))
    red.stage_c(n_u - 2)
    relay_to(step(1, min(6, n_f1 - 2)))
    peer_to(step(1, n_f1))
    red.stage_d(n_u - 3, *units[n_u - 3])
    red.stage_c(n_u - 1)
    red.stage_d(n_u - 2, *units[n_u - 2])
    mate_to(step(1, n_f1))
    settle(D.n_o - 1)
    red.stage_d(n_u - 1, *units[n_u - 1])
    settle(D.n_o)
    red.finish(n_u)

    def slice_of(d):
        return hid.at[rows_at(d * dl, dl), :]

    own_y = pltpu.make_async_copy(slice_of(me), piece_of(y_out, me), xr.at[0])

    def y_copy_back(i):
        d = lax.rem(me + i, n)
        return remote(slice_of(d), piece_of(y_out, me), xs.at[i], xr.at[i], d // n_col, lax.rem(d, n_col))

    def y_send_back(i):
        @pl.when(i == 0)
        def _():
            own_y.start()

        @pl.when(i != 0)
        def _():
            y_copy_back(i).start()

    def y_finish(i):
        s = lax.rem(me + n - i, n)
        remote(piece_of(y_out, s), piece_of(y_out, s), xs.at[i], xr.at[i], row, col).wait_recv()
        y_copy_back(i).wait_send()

    def y_ready(low, high):
        def body(i):
            d = lax.rem(me + i, n)
            r, a = d // n_col, lax.rem(d, n_col) * dl
            first = lax.rem(a // och + D.n_o - lax.rem(r, D.n_o), D.n_o)
            second = lax.rem((a + dl - 1) // och + D.n_o - lax.rem(r, D.n_o), D.n_o)

            done = jnp.maximum(first, second)

            @pl.when((low <= done) & (done < high))
            def _():
                y_send_back(i)

        loop(0, n, body)

    for l in range(1, D.layers):
        C = D.cfg[l]
        layer_norm(l)
        g0 = Gather(normed_of(ht), 0)
        peer_to(step(l, C.n_f))
        mate_to(step(l, C.n_f))
        relay_to(step(l, min(8, C.n_f)))
        own1, near2 = (lambda i: x), (lambda i: lax.rem(x + 1 + 2 * i, n_x))
        n_mid = min(3, C.n_c - 1)

        def begin(seq_of, count):
            load_q(l)
            have_chunk(l, 0)
            start(w_fetch(l, "f", 0, 0))
            project_q(l, 0, seq_of, count)

        g0.own()
        begin(own1, 1)
        gate_up_loop(l, 0, own1, 1, 0, n_mid, n_mid)
        g0.pass_low()
        relay_to(step(l, C.n_f))
        peer_to(step(l, C.n_f + 2))
        mate_to(step(l, C.n_f + 2))
        g0.pass_on()
        g0.near()
        begin(near2, 2)
        gate_up_loop(l, 0, near2, 2, 0, n_mid)
        g0.pass_far()
        kv_send(near3, 3)
        relay_to(step(l, C.n_f + 1))
        peer_to(step(l, C.n_f + 4))
        mate_to(step(l, C.n_f + 4))
        gate_up_loop(l, 0, near3, 3, n_mid, C.n_c)
        relay_to(step(l, C.n_f + 2))
        g0.far()
        begin(far1, 1)
        kv_send(far1, 1)
        gate_up_loop(l, 0, far1, 1, 0, C.n_c)
        peer_to(step(l, C.n_f + D.n_o))
        mate_to(step(l, C.n_f + D.n_o))
        relay_to(step(l, C.n_f + 3))
        g0.finish()
        kv_arrive()
        key_value(l, 0)
        o_load(l, 0, 0)
        attention(l, 0)
        relay_to(step(l, C.n_f + 4))
        red = Reduce(l)
        last = l + 1 == D.layers

        end = D.n_o - 1
        for j in range(D.n_o):
            o_use(l, j, 0)
            red.stage_a(j, 0)
            if j == 1:
                relay_to(step(l, C.n_f + D.n_o))
            if j < end:
                o_load(l, j + 1, 0)
            if 2 <= j:
                red.stage_c(j - 2)
            if 3 <= j:
                red.stage_d(j - 3, j - 3, 0)
            red.stage_b(j)
        red.stage_c(end - 1)
        red.stage_d(end - 2, end - 2, 0)
        red.stage_c(end)
        red.stage_d(end - 1, end - 1, 0)
        if last:
            with sc("send"):
                y_ready(0, end)
        red.stage_d(end, end, 0)
        if last:
            y_ready(end, end + 1)
        red.finish(D.n_o)

    def kv_back(i):
        r = lax.rem(row + i, n_row)
        pos = rows_at((r * n_col + col) * D.pos, D.pos)
        return kvbuf.at[:, :, :, pos, :], kv_out.at[:, :, pl.ds(row * D.seqs, D.seqs)], r

    src, dst, _ = kv_back(0)
    own_kv = pltpu.make_async_copy(src, dst, fl)
    own_kv.start()
    kv_sends = []
    for i in range(1, n_row):
        src, dst, r = kv_back(i)
        c = remote(src, dst, fs.at[i], fr.at[i], r, col)
        c.start()
        kv_sends.append(c)

    with sc("ywait"):
        loop(1, n, y_finish)
        own_y.wait()
        own_kv.wait()
        for i in range(1, n_row):
            r = lax.rem(row + n_row - i, n_row)
            dst = kv_out.at[:, :, pl.ds(r * D.seqs, D.seqs)]
            remote(dst, dst, fs.at[i], fr.at[i], row, col).wait_recv()
        for c in kv_sends:
            c.wait_send()
        for c in y_sent:
            c.wait_send()


def solution(mesh):
    n_row, n_col = mesh.shape["row"], mesh.shape["col"]
    group = n_row * n_col
    act_spec = P("dp", None, ("row", "col"))
    weight_spec = P(None, "row", "col")

    def device_fn(x_loc, gain_loc, w_in_loc, w_kv_loc, w_out_loc):
        D = Dims()
        D.n_row, D.n_col = n_row, n_col
        n_batch, D.seq, D.dl = x_loc.shape
        D.layers, D.dr, e = w_in_loc.shape
        D.d = D.dl * group
        r_block = w_out_loc.shape[1]
        D.f = e - r_block
        D.q = r_block - D.f
        kv_local = w_kv_loc.shape[2]
        D.hd = kv_local * n_col // 2
        D.kvp = 32
        D.tok = n_batch * D.seq // group
        D.seqs = n_batch // n_row
        D.pos = D.seq // group
        D.fch = 128
        D.och = 128
        D.n_o = D.dr // D.och
        D.cfg = []
        for l in range(D.layers):
            C = Dims()
            C.split = l == 0
            parts = 2 if C.split else 1
            C.q, C.f = D.q // parts, D.f // parts
            C.heads, C.n_f = C.q // D.hd, C.f // D.fch
            C.cw = D.fch if C.split else 2 * D.fch
            C.n_c = C.f // C.cw
            D.cfg.append(C)
        assert D.seq == 2 * D.tok and D.seqs == n_col // 2 == n_row == 4

        half = D.hd // 2
        inv_freq = (np.float32(1.0) / (np.float32(10000.0) ** (np.arange(half, dtype=np.float32) * np.float32(2.0) / np.float32(D.hd)))).astype(np.float32)
        angles = (inv_freq[:, None] * np.arange(D.seq, dtype=np.float32)[None, :]).astype(np.float32)
        cos_t, sin_t = np.cos(angles).astype(np.float32), np.sin(angles).astype(np.float32)
        perm = np.zeros((2 * D.hd, n_col * D.kvp), np.float32)
        for i in range(2 * D.hd):
            perm[i, (i // kv_local) * D.kvp + i % kv_local] = 1.0

        x_t = x_loc.transpose(0, 2, 1)
        w_t = w_in_loc.transpose(0, 2, 1)
        wkv_t = jnp.pad(w_kv_loc.transpose(0, 2, 1), ((0, 0), (0, D.kvp - kv_local), (0, 0)))
        gains = jnp.pad(gain_loc, ((0, 16 - D.layers), (0, 128 - D.dl)))

        n_y = sum(12 + 6 * (C.n_f + D.n_o) for C in D.cfg)
        m = D.och * n_row
        sds = jax.ShapeDtypeStruct
        dma = pltpu.SemaphoreType.DMA
        out = pl.pallas_call(
            functools.partial(kernel, D),
            out_shape=(
                sds(x_t.shape, BF16),
                sds((D.layers, 2, n_batch, D.pos, 128), BF16),
                sds((D.layers, e, D.d), BF16),
                sds((D.layers, D.kvp, D.d), BF16),
                sds((D.layers, n_row, r_block, D.dr), BF16),
                sds((D.seqs, D.d, D.seq), BF16),
            ),
            in_specs=[ANY] * 5 + [VMEM] * 3,
            out_specs=(ANY,) * 6,
            scratch_shapes=[
                pltpu.VMEM((group, D.dl, D.tok), BF16),
                pltpu.VMEM((group, 16, 128), BF16),
                pltpu.VMEM((D.layers, D.d, 128), F32),
                pltpu.VMEM((D.d, D.tok), BF16),
                pltpu.VMEM((D.seqs, D.d, D.seq), BF16),
                pltpu.VMEM((2, max(4 * D.fch, D.q + D.kvp), D.d), BF16),
                pltpu.VMEM((2, r_block, m), BF16),
                pltpu.VMEM((m, r_block), BF16),
                pltpu.VMEM((D.seqs * D.q, D.seq), BF16),
                pltpu.VMEM((n_col, 2 * D.seqs, D.kvp, D.seq), BF16),
                pltpu.VMEM((2 * D.seqs, D.seq, 128), BF16),
                pltpu.VMEM((2 * D.seqs, D.hd, D.seq), BF16),
                pltpu.VMEM((D.layers, 2, D.seqs, D.seq, 128), BF16),
                pltpu.VMEM((D.seqs * r_block, D.seq), BF16),
                pltpu.VMEM((2, D.seqs, m, D.seq), BF16),
                pltpu.VMEM((5, 4, m, D.tok), BF16),
                pltpu.VMEM((5, m, D.tok), BF16),
                pltpu.VMEM((5, 2, m, D.tok), BF16),
                pltpu.VMEM((2, D.n_o, m, D.tok), BF16),
                pltpu.VMEM((D.n_o, m, D.tok), BF16),
                dma((group,)), dma((group,)), dma((group,)), dma((group,)),
                dma((n_y,)), dma((n_y,)),
                dma((4, 13)), dma((4, 13)), dma, dma,
                dma((D.seqs, n_col)), dma((D.seqs, n_col)),
                dma((5, 8)), dma((5, 8)),
                dma((D.n_o,)), dma((D.n_o,)),
                dma((2, 8)), dma((2, 8)), dma((D.seqs,)),
                dma((n_row,)), dma((n_row,)), dma,
            ],
            compiler_params=pltpu.CompilerParams(collective_id=0, has_side_effects=True, vmem_limit_bytes=67_000_000),
            name="two_layers",
        )(x_t, gains, w_t, wkv_t, w_out_loc, jnp.asarray(cos_t), jnp.asarray(sin_t), jnp.asarray(perm, BF16))
        return out[0].transpose(0, 2, 1), out[1][..., : D.hd]

    return jax.shard_map(device_fn, mesh=mesh, in_specs=(act_spec, P(None, ("row", "col")), weight_spec, weight_spec, P(None, "col", "row")), out_specs=(act_spec, P(None, None, "dp", ("row", "col"), None)), check_vma=False)
```

profile of v0, /device:TPU:97, one launch (start us, length us, event | category | flops | bytes accessed | tf_op | source)
XLA Modules:
  0.0 412.7 jit_solution(11837652079262783417)
XLA Ops:
  0.6 1.3 pad.8.gains
  1.9 0.8 copy.12
  2.7 0.6 pad.9.wkv_t
  3.3 405.2 %two_layers.1 = (bf16[16,80,512]{2,1,0:T(8,128)(2,1)}, bf16[2,2,16,16,128]{4,3,2,1,0:T(8,128)(2,1)}, bf16[2,2880,2560]{2,1,0:T(8,128)(2,1)}, bf16[2,32,2560]{2,1...) custom-call(bf16[16,80,512]{2,1,0:T(8,128)(2,1)} %bitcast.8, ...), custom_call_target="tpu_custom_call" | custom-call | tf_op jit(solution)/shard_map/two_layers/pallas_call | solution.py:1030
  408.6 2.5 copy.15
  411.0 1.7 copy.16
where the time goes:
time: 420 us; the launch traced here: 413 us
  Pallas kernels  405 us (96%)
  local copies, waits for them, and re-layouts  6.84 us (2%)
    pallas_call x1, Pallas kernels, device_fn(): pl.pallas_call(functools.partial(kernel, D), out_shape=(sds(x_t.shape, BF...  405 us

commit v1 on v0

--- a/solution.py
+++ b/solution.py
@@ -799,7 +799,7 @@
             kv1.pass_on()
         gate_up_loop(0, 1, all4, 4, cuts[u - 2], cuts[u - 1])
     kv1.pass_far()
-    relay_to(step(1, 1))
+    relay_to(step(1, 0))
     with sc("kv1wait"):
         kv1.own()
         kv1.near()
@@ -808,14 +808,13 @@
     key_value(0, 1)
     attention(0, 1)
     g1.finish()
-    relay_to(step(1, 2))
     peer_to(step(1, 7))
     n_f1 = D.cfg[1].n_f
     for u in range(first, n_u):
         unit(u)
         v = u - first
-        if v in (0, 1, 2):
-            relay_to(step(1, min(v + 3, n_f1 - 2)))
+        if v in (0, 1, 2, 3):
+            relay_to(step(1, min(v + 2, n_f1 - 2)))
         if v == 1:
             peer_to(step(1, min(8, n_f1)))
         elif v == 4:

time: 420 us -> 416 us (level)
  no operation moved by 1% of the time
where the time goes in v1:
time: 416 us; the launch traced here: 411 us
  Pallas kernels  404 us (97%)
  local copies, waits for them, and re-layouts  6.84 us (2%)
    pallas_call x1, Pallas kernels, device_fn(): pl.pallas_call(functools.partial(kernel, D), out_shape=(sds(x_t.shape, BF...  404 us

profile of v1, /device:TPU:97, one launch (start us, length us, event | category | flops | bytes accessed | tf_op | source)
XLA Modules:
  0.0 411.4 jit_solution(9396594870204884337)
XLA Ops:
  0.6 1.3 pad.8.gains
  1.9 0.8 copy.12
  2.7 0.6 pad.9.wkv_t
  3.3 404.0 %two_layers.1 = (bf16[16,80,512]{2,1,0:T(8,128)(2,1)}, bf16[2,2,16,16,128]{4,3,2,1,0:T(8,128)(2,1)}, bf16[2,2880,2560]{2,1,0:T(8,128)(2,1)}, bf16[2,32,2560]{2,1...) custom-call(bf16[16,80,512]{2,1,0:T(8,128)(2,1)} %bitcast.8, ...), custom_call_target="tpu_custom_call" | custom-call | tf_op jit(solution)/shard_map/two_layers/pallas_call | solution.py:1029
  407.3 2.5 copy.15
  409.8 1.7 copy.16
